TPU v7x, 256 devices: a whole 4x4x8 slice. The times are simulated.
256 devices in a mesh: dp: 32 (over y, x, core), seq: 8 (over z).
Axes of the slice: x: 4, y: 4, z: 8, core: 2. Of those that a mesh axis runs over, the one named last changes fastest.
Arguments:
- query_rows: bfloat16 [32, 1024, 3072], P('dp', 'seq'), may hold values from -6 to 6
- key_rows: bfloat16 [32, 1024, 3072], P('dp', 'seq'), may hold values from -6 to 6
- value_rows: bfloat16 [32, 1024, 3072], P('dp', 'seq'), may hold values from -6 to 6
- out_grad: bfloat16 [32, 1024, 6144], P('dp', 'seq'), may hold values from -54 to 54
- clip_lengths: int32 [32, 4], P('dp'), may hold values from 1 to 512, 1024 in all within a row
- out_weight: bfloat16 [3072, 6144], P('seq'), may hold values from -0.109375 to 0.109375
- query_gain: float32 [128], replicated, may hold values from 0.1 to 1.9
- key_gain: float32 [128], replicated, may hold values from 0.1 to 1.9
Outputs:
- query_grad: bfloat16 [32, 1024, 3072], P('dp', 'seq')
- key_grad: bfloat16 [32, 1024, 3072], P('dp', 'seq')
- value_grad: bfloat16 [32, 1024, 3072], P('dp', 'seq')
- weight_grad: float32 [3072, 6144], P('seq', 'dp')
- querygain_grad: float32 [128], replicated
- keygain_grad: float32 [128], replicated
- grad_norm: float32 [], replicated
Inputs may be any that keep to these rules, and one draw needn't show every extreme that they name: `clip_lengths`: the token counts of each group's clips sum to 1024.
All inputs are finite; a program needn't handle non-finite values.
Results may differ from a plain program's by a relative error of at most 0.015.
Values may be sent and summed in bfloat16 or wider, within the bound.
A program may use at most 128 MiB of HBM per device.

v0:
```python
import jax
import jax.numpy as jnp
from jax import lax
from jax.sharding import Mesh
from jax.sharding import PartitionSpec as P

HEAD_DIM = 128
MAX_NORM = 768
DP = ("dp_0", "dp_1", "dp_2")
DP_SEQ = ("dp_0", "dp_1", "dp_2", "seq")
EPS = 1e-06


def one_axis_at_a_time(array, axes):
    for axis in axes:
        array = lax.psum(array, axis)
    return array


def segment_ids(lengths, total):
    ends = jnp.cumsum(lengths)
    places = jnp.arange(total, dtype=jnp.int32)
    return jnp.sum((places[:, None] >= ends[None, :]).astype(jnp.int32), axis=1)


def norm_rows(rows, gain):
    wide = rows.astype(jnp.float32)
    inverse = lax.rsqrt(jnp.mean(wide * wide, axis=-1, keepdims=True) + EPS)
    unit = wide * inverse
    return (unit, inverse, (unit * gain).astype(jnp.bfloat16))


def norm_back(unit, inverse, gain, d_norm):
    gain_part = jnp.sum(unit * d_norm, axis=(0, 1))
    d_unit = d_norm * gain
    d_rows = inverse * (d_unit - unit * jnp.mean(unit * d_unit, axis=-1, keepdims=True))
    return (d_rows.astype(jnp.bfloat16), gain_part)


def local(
    query_rows, key_rows, value_rows, out_grad, clip_lengths, out_weight, query_gain, key_gain
):
    query, keys, values = (
        lax.all_to_all(query_rows[0], "seq", split_axis=1, concat_axis=0, tiled=True),
        lax.all_to_all(key_rows[0], "seq", split_axis=1, concat_axis=0, tiled=True),
        lax.all_to_all(value_rows[0], "seq", split_axis=1, concat_axis=0, tiled=True),
    )
    total = query.shape[0]
    heads = query.shape[1] // HEAD_DIM
    width = heads * HEAD_DIM
    scale = HEAD_DIM ** (-0.5)
    block = min(512, total)
    blocks = total // block
    seg = segment_ids(clip_lengths[0], total)
    q_unit, q_inv, q_norm = norm_rows(query.reshape(total, heads, HEAD_DIM), query_gain)
    k_unit, k_inv, k_norm = norm_rows(keys.reshape(total, heads, HEAD_DIM), key_gain)
    values3 = values.reshape(total, heads, HEAD_DIM)

    def forward_block(index):
        start = index * block
        query_block = lax.dynamic_slice_in_dim(q_norm, start, block, 0)
        seg_block = lax.dynamic_slice_in_dim(seg, start, block, 0)
        scores = (
            jnp.einsum("qhd,khd->hqk", query_block, k_norm, preferred_element_type=jnp.float32)
            * scale
        )
        same = seg_block[:, None] == seg[None, :]
        expo = jnp.where(same[None], jnp.exp(scores), 0.0)
        probs = (expo / jnp.sum(expo, axis=-1, keepdims=True)).astype(jnp.bfloat16)
        attn_out = jnp.einsum("hqk,khd->qhd", probs, values3, preferred_element_type=jnp.float32)
        return (probs, attn_out.astype(jnp.bfloat16))

    probs_all, attn_blocks = lax.map(forward_block, jnp.arange(blocks, dtype=jnp.int32))
    attn_flat = attn_blocks.reshape(total, width)
    out_full = lax.all_gather(out_grad[0], "seq", axis=0, tiled=True)
    weight_part = jnp.dot(attn_flat.T, out_full, preferred_element_type=jnp.float32)
    d_attn = jnp.dot(out_full, out_weight.T, preferred_element_type=jnp.float32).astype(
        jnp.bfloat16
    )
    d_attn3 = d_attn.reshape(total, heads, HEAD_DIM)

    def backward_block(carry, items):
        d_key, d_value = carry
        probs, index = items
        start = index * block
        attn_grad = lax.dynamic_slice_in_dim(d_attn3, start, block, 0)
        query_block = lax.dynamic_slice_in_dim(q_norm, start, block, 0)
        d_probs = jnp.einsum("qhd,khd->hqk", attn_grad, values3, preferred_element_type=jnp.float32)
        probs32 = probs.astype(jnp.float32)
        row_sum = jnp.sum(probs32 * d_probs, axis=-1, keepdims=True)
        d_scores = (probs32 * (d_probs - row_sum) * scale).astype(jnp.bfloat16)
        d_value = d_value + jnp.einsum(
            "hqk,qhd->khd", probs, attn_grad, preferred_element_type=jnp.float32
        )
        d_key = d_key + jnp.einsum(
            "hqk,qhd->khd", d_scores, query_block, preferred_element_type=jnp.float32
        )
        d_query = jnp.einsum("hqk,khd->qhd", d_scores, k_norm, preferred_element_type=jnp.float32)
        return ((d_key, d_value), d_query)

    empty = jnp.zeros((total, heads, HEAD_DIM), jnp.float32)
    (d_knorm, d_value32), d_query_blocks = lax.scan(
        backward_block, (empty, empty), (probs_all, jnp.arange(blocks, dtype=jnp.int32))
    )
    d_qnorm = d_query_blocks.reshape(total, heads, HEAD_DIM)
    query_grad, q_gain_part = norm_back(q_unit, q_inv, query_gain, d_qnorm)
    key_grad, k_gain_part = norm_back(k_unit, k_inv, key_gain, d_knorm)
    value_grad = d_value32.astype(jnp.bfloat16)
    query_back, key_back, value_back = (
        lax.all_to_all(
            query_grad.reshape(total, width), "seq", split_axis=0, concat_axis=1, tiled=True
        ),
        lax.all_to_all(
            key_grad.reshape(total, width), "seq", split_axis=0, concat_axis=1, tiled=True
        ),
        lax.all_to_all(
            value_grad.reshape(total, width), "seq", split_axis=0, concat_axis=1, tiled=True
        ),
    )
    weight_shard = lax.psum_scatter(
        weight_part.astype(jnp.bfloat16), DP, scatter_dimension=1, tiled=True
    ).astype(jnp.float32)
    local_squares = jnp.sum(weight_shard * weight_shard)
    qgain_raw, kgain_raw = (
        one_axis_at_a_time(q_gain_part, DP_SEQ),
        one_axis_at_a_time(k_gain_part, DP_SEQ),
    )
    weight_squares = one_axis_at_a_time(local_squares, DP_SEQ)
    squares = weight_squares + jnp.sum(qgain_raw * qgain_raw) + jnp.sum(kgain_raw * kgain_raw)
    grad_norm = jnp.sqrt(squares)
    factor = jnp.minimum(jnp.float32(1.0), MAX_NORM / (grad_norm + EPS))
    return (
        query_back[None],
        key_back[None],
        value_back[None],
        weight_shard * factor,
        qgain_raw * factor,
        kgain_raw * factor,
        grad_norm,
    )


def solution(mesh):
    torus = Mesh(mesh.devices.reshape(4, 4, 2, mesh.shape["seq"]), ("dp_0", "dp_1", "dp_2", "seq"))
    return jax.shard_map(
        local,
        mesh=torus,
        in_specs=(
            P(DP, "seq", None),
            P(DP, "seq", None),
            P(DP, "seq", None),
            P(DP, "seq", None),
            P(DP, None),
            P("seq", None),
            P(),
            P(),
        ),
        out_specs=(
            P(DP, "seq", None),
            P(DP, "seq", None),
            P(DP, "seq", None),
            P("seq", DP),
            P(),
            P(),
            P(),
        ),
        check_vma=False,
    )
```

profile of v0, /device:TPU:32, one launch (start us, length us, event | category | flops | bytes accessed | tf_op | source)
XLA Modules:
  0.0 430.5 jit_solution(6281215837916845542)
XLA Ops:
  9.5 8.6 %all-to-all-start = ((bf16[128,8,384]{0,2,1:T(8,128)(2,1)}), bf16[128,8,384]{0,2,1:T(8,128)(2,1)S(1)}, u32[]{:S(2)}, u32[]{:S(2)}) async-start(bf16[128,8,384]{0,2,1:T(8,128)(2,1)} %bitcast.4), calls=%async_computation | async-start | bytes 1572864 | tf_op jit(solution)/shard_map/all_to_all | solution.py:44
  19.2 26.2 %all-to-all-done = bf16[128,8,384]{0,2,1:T(8,128)(2,1)S(1)} async-done(((bf16[128,8,384]{0,2,1:T(8,128)(2,1)}), bf16[128,8,384]{0,2,1:T(8,128)(2,1)S(1)}, u32[]{:S(2)}, u32[]{:S(2)}) %all-to-all-start) | async-done | bytes 786464 | tf_op jit(solution)/shard_map/all_to_all | solution.py:44
  45.4 5.8 %all-to-all-start.1 = ((bf16[128,8,384]{0,2,1:T(8,128)(2,1)}), bf16[128,8,384]{0,2,1:T(8,128)(2,1)S(1)}, u32[]{:S(2)}, u32[]{:S(2)}) async-start(bf16[128,8,384]{0,2,1:T(8,128)(2,1)} %bitcast.8), calls=%async_computation.1 | async-start | bytes 1572864 | tf_op jit(solution)/shard_map/all_to_all | solution.py:45
  52.3 30.0 %all-to-all-done.1 = bf16[128,8,384]{0,2,1:T(8,128)(2,1)S(1)} async-done(((bf16[128,8,384]{0,2,1:T(8,128)(2,1)}), bf16[128,8,384]{0,2,1:T(8,128)(2,1)S(1)}, u32[]{:S(2)}, u32[]{:S(2)}) %all-to-all-start.1) | async-done | bytes 786464 | tf_op jit(solution)/shard_map/all_to_all | solution.py:45
  82.4 5.3 %all-to-all-start.2 = ((bf16[128,8,384]{0,2,1:T(8,128)(2,1)}), bf16[128,8,384]{0,2,1:T(8,128)(2,1)}, u32[]{:S(2)}, u32[]{:S(2)}) async-start(bf16[128,8,384]{0,2,1:T(8,128)(2,1)} %bitcast.10), calls=%async_computation.2 | async-start | bytes 1572864 | tf_op jit(solution)/shard_map/all_to_all | solution.py:46
  92.0 2.1 copy.147
  97.4 2.3 copy.151
  99.7 19.1 %all-to-all-done.2 = bf16[128,8,384]{0,2,1:T(8,128)(2,1)} async-done(((bf16[128,8,384]{0,2,1:T(8,128)(2,1)}), bf16[128,8,384]{0,2,1:T(8,128)(2,1)}, u32[]{:S(2)}, u32[]{:S(2)}) %all-to-all-start.2) | async-done | bytes 786464 | tf_op jit(solution)/shard_map/all_to_all | solution.py:46
  118.7 2.5 copy.149
  121.2 2.2 reshape.177
  123.4 2.3 copy.152
  128.8 21.1 %while.27 = (s32[]{:T(128)}, bf16[2,3,512,1024]{3,2,1,0:T(8,128)(2,1)}, bf16[2,512,3,128]{3,1,2,0:T(8,128)(2,1)}, s32[2]{0:T(128)S(1)}, s32[1024]{0:T(1024)S(1)}...) while((s32[]{:T(128)}, ...), condition=%wide.region_6.7_spmd, body=%wide.region_4.6_spmd.sunk | while | flops 817035776 | bytes 85746000 | solution.py:73
  130.5 3.4 fusion.75
  141.1 3.4 fusion.75
  149.9 3.1 copy.167
  153.0 2.1 copy.180
  156.8 32.1 %all-gather.3.cloned.1.call-done = bf16[1,1024,6144]{2,1,0:T(8,128)(2,1)} async-done(((bf16[1,128,6144]{2,1,0:T(8,128)(2,1)}), bf16[1,1024,6144]{2,1,0:T(8,128)(2,1)}) %all-gather.3.cloned.1.call-update) | async-done | bytes 12582928 | tf_op jit(solution)/shard_map/all_gather | solution.py:75
  188.9 11.4 %fusion.42 = bf16[384,6144]{0,1:T(8,128)(2,1)} fusion(bf16[1024,384]{0,1:T(8,128)(2,1)} %bitcast.161, bf16[1,1024,6144]{2,1,0:T(8,128)(2,1)} %all-gather.3.cloned.1.call-done), kind=kOutput, calls=%fused_computation.45 | convolution fusion | flops 4834197504 | bytes 18087936 | tf_op jit(solution)/shard_map/dot_general | solution.py:76
  200.3 10.4 %fusion.48 = bf16[1024,384]{0,1:T(8,128)(2,1)} fusion(bf16[384,6144]{1,0:T(8,128)(2,1)} %param.17, bf16[1,1024,6144]{2,1,0:T(8,128)(2,1)} %all-gather.3.cloned.1.call-done), kind=kOutput, calls=%fused_computation.62 | convolution fusion | flops 4832231424 | bytes 18087936 | tf_op jit(solution)/shard_map/dot_general | solution.py:77
  210.8 57.7 %while.28 = (s32[]{:T(128)}, f32[1024,3,128]{0,2,1:T(8,128)}, f32[1024,3,128]{0,2,1:T(8,128)S(1)}, f32[2,512,3,128]{3,1,2,0:T(8,128)}, s32[2]{0:T(128)S(1)}, /*i...) while((s32[]{:T(128)}, f32[1024,3,128]{0,2,1:T(8,128)}, ...), condition=%wide.region_9.10_spmd.clone, body=%wide.region_7.9_spmd.clone.sunk | while | flops 1634210816 | bytes 57019604 | solution.py:102
  212.0 5.0 %fusion.83 = f32[3,512,1024]{2,1,0:T(8,128)} fusion(bf16[1024,3,128]{2,0,1:T(8,128)(2,1)} %get-tuple-element.549, bf16[1024,3,128]{0,2,1:T(8,128)(2,1)} %get-tuple-element.548, s32[]{:T(128)S(6)} %select_n.24), kind=kOutput, calls=%fused_computation.30.clone.1 | convolution fusion | flops 402653184 | bytes 7471108 | tf_op jit(solution)/shard_map/while/body/eval_jaxpr/qhd,khd->hqk/dot_general | solution.py:88
  217.0 10.2 %bitcast_add_fusion.4 = f32[1024,3,128]{0,2,1:T(8,128)} fusion(f32[1024,3,128]{0,2,1:T(8,128)} %get-tuple-element.528, f32[3,512,1024]{2,1,0:T(8,128)} %fusion.83, bf16[2,3,512,1024]{3,2,1,0:T(8,128)(2,1)} %get-tuple-element.547, s32[]{:T(128)} %get-tuple-element.527, pred[]{:T(512)S(6)} %compare.3, bf16[1024,3,128]{0,2,1:T(8,128)(2,1)} %get-tuple-element.546, ...), kind=kOutput, calls=%fused_computation.26.clone.1 | convolution fusion | flops 414452224 | bytes 22414340 | tf_op jit(solution)/shard_map/while/body/eval_jaxpr/hqk,qhd->khd/dot_general | solution.py:95
  227.2 9.7 %fusion.84 = f32[2,512,3,128]{3,1,2,0:T(8,128)} fusion(f32[2,512,3,128]{3,1,2,0:T(8,128)} %get-tuple-element.530, s32[]{:T(128)} %get-tuple-element.527, bf16[1024,3,128]{2,0,1:T(8,128)(2,1)} %get-tuple-element.550, f32[3,512,1024]{2,1,0:T(8,128)} %fusion.83, bf16[2,3,512,1024]{3,2,1,0:T(8,128)(2,1)} %get-tuple-element.547), kind=kOutput, calls=%fused_computation.28.clone.1 | convolution fusion | flops 413665792 | bytes 20448768 | tf_op jit(solution)/shard_map/while/body/eval_jaxpr/hqk,khd->qhd/dot_general | solution.py:98
  236.9 3.0 bitcast_add_fusion.5
  241.2 4.9 %fusion.83 = f32[3,512,1024]{2,1,0:T(8,128)} fusion(bf16[1024,3,128]{2,0,1:T(8,128)(2,1)} %get-tuple-element.549, bf16[1024,3,128]{0,2,1:T(8,128)(2,1)} %get-tuple-element.548, s32[]{:T(128)S(6)} %select_n.24), kind=kOutput, calls=%fused_computation.30.clone.1 | convolution fusion | flops 402653184 | bytes 7471108 | tf_op jit(solution)/shard_map/while/body/eval_jaxpr/qhd,khd->hqk/dot_general | solution.py:88
  246.1 10.1 %bitcast_add_fusion.4 = f32[1024,3,128]{0,2,1:T(8,128)} fusion(f32[1024,3,128]{0,2,1:T(8,128)} %get-tuple-element.528, f32[3,512,1024]{2,1,0:T(8,128)} %fusion.83, bf16[2,3,512,1024]{3,2,1,0:T(8,128)(2,1)} %get-tuple-element.547, s32[]{:T(128)} %get-tuple-element.527, pred[]{:T(512)S(6)} %compare.3, bf16[1024,3,128]{0,2,1:T(8,128)(2,1)} %get-tuple-element.546, ...), kind=kOutput, calls=%fused_computation.26.clone.1 | convolution fusion | flops 414452224 | bytes 22414340 | tf_op jit(solution)/shard_map/while/body/eval_jaxpr/hqk,qhd->khd/dot_general | solution.py:95
  256.2 9.3 %fusion.84 = f32[2,512,3,128]{3,1,2,0:T(8,128)} fusion(f32[2,512,3,128]{3,1,2,0:T(8,128)} %get-tuple-element.530, s32[]{:T(128)} %get-tuple-element.527, bf16[1024,3,128]{2,0,1:T(8,128)(2,1)} %get-tuple-element.550, f32[3,512,1024]{2,1,0:T(8,128)} %fusion.83, bf16[2,3,512,1024]{3,2,1,0:T(8,128)(2,1)} %get-tuple-element.547), kind=kOutput, calls=%fused_computation.28.clone.1 | convolution fusion | flops 413665792 | bytes 20448768 | tf_op jit(solution)/shard_map/while/body/eval_jaxpr/hqk,khd->qhd/dot_general | solution.py:98
  265.5 2.9 bitcast_add_fusion.5
  268.5 3.7 copy.156
  272.2 2.7 copy.159
  274.9 3.0 copy.160
  277.9 2.3 multiply_reduce_fusion.3
  281.9 3.3 reshape.179
  285.3 4.3 fusion.47
  289.5 6.7 %all-to-all-start.3 = ((bf16[8,128,384]{1,2,0:T(8,128)(2,1)}), bf16[8,128,384]{1,2,0:T(8,128)(2,1)}, u32[]{:S(2)}, u32[]{:S(2)}) async-start(bf16[8,128,384]{1,2,0:T(8,128)(2,1)} %fusion.47), calls=%async_computation.3 | async-start | bytes 1572864 | tf_op jit(solution)/shard_map/all_to_all | solution.py:110
  296.2 2.0 multiply_reduce_fusion
  300.3 17.9 %all-to-all-done.3 = bf16[8,128,384]{1,2,0:T(8,128)(2,1)} async-done(((bf16[8,128,384]{1,2,0:T(8,128)(2,1)}), bf16[8,128,384]{1,2,0:T(8,128)(2,1)}, u32[]{:S(2)}, u32[]{:S(2)}) %all-to-all-start.3) | async-done | bytes 786464 | tf_op jit(solution)/shard_map/all_to_all | solution.py:110
  318.2 4.9 %all-to-all-start.4 = ((bf16[8,128,384]{2,1,0:T(8,128)(2,1)}), bf16[8,128,384]{2,1,0:T(8,128)(2,1)S(1)}, u32[]{:S(2)}, u32[]{:S(2)}) async-start(bf16[8,128,384]{2,1,0:T(8,128)(2,1)} %copy.163), calls=%async_computation.4 | async-start | bytes 1572864 | tf_op jit(solution)/shard_map/all_to_all | solution.py:113
  324.8 18.6 %all-to-all-done.4 = bf16[8,128,384]{2,1,0:T(8,128)(2,1)S(1)} async-done(((bf16[8,128,384]{2,1,0:T(8,128)(2,1)}), bf16[8,128,384]{2,1,0:T(8,128)(2,1)S(1)}, u32[]{:S(2)}, u32[]{:S(2)}) %all-to-all-start.4) | async-done | bytes 786464 | tf_op jit(solution)/shard_map/all_to_all | solution.py:113
  343.4 5.5 %all-to-all-start.5 = ((bf16[8,128,384]{2,1,0:T(8,128)(2,1)}), bf16[8,128,384]{2,1,0:T(8,128)(2,1)}, u32[]{:S(2)}, u32[]{:S(2)}) async-start(bf16[8,128,384]{2,1,0:T(8,128)(2,1)} %copy.165), calls=%async_computation.5 | async-start | bytes 1572864 | tf_op jit(solution)/shard_map/all_to_all | solution.py:116
  349.0 1.9 reshape.184
  350.9 2.6 multiply_reduce_fusion.1
  353.6 2.4 copy.170
  357.5 11.9 %all-to-all-done.5 = bf16[8,128,384]{2,1,0:T(8,128)(2,1)} async-done(((bf16[8,128,384]{2,1,0:T(8,128)(2,1)}), bf16[8,128,384]{2,1,0:T(8,128)(2,1)}, u32[]{:S(2)}, u32[]{:S(2)}) %all-to-all-start.5) | async-done | bytes 786464 | tf_op jit(solution)/shard_map/all_to_all | solution.py:116
  373.6 13.2 %all-reduce.2 = (f32[]{:T(128)}, f32[128]{0:T(128)S(1)}, f32[128]{0:T(128)S(1)}) all-reduce(f32[]{:T(128)} %fusion.51, f32[128]{0:T(128)S(1)} %multiply_reduce_fusion.1, f32[128]{0:T(128)S(1)} %get-tuple-element.303), channel_id=1, replica_groups=mesh['dp_0'=4,'dp_1'=4,'dp_2'=2,'seq'=8] {'dp_0'}, use_global_device_ids=true, to_apply=%region_14.15 | all-reduce | flops 257 | bytes 2056 | tf_op jit(solution)/shard_map/psum | solution.py:16
  386.9 11.0 %all-reduce.1 = (f32[]{:T(128)}, f32[128]{0:T(128)S(1)}, f32[128]{0:T(128)S(1)}) all-reduce(f32[]{:T(128)} %get-tuple-element.347, f32[128]{0:T(128)S(1)} %get-tuple-element.348, f32[128]{0:T(128)S(1)} %get-tuple-element.349), channel_id=1, replica_groups=mesh['dp_0'=4,'dp_1'=4,'dp_2'=2,'seq'=8] {'dp_1'}, use_global_device_ids=true, to_apply=%region_15.16 | all-reduce | flops 257 | bytes 2056 | tf_op jit(solution)/shard_map/psum | solution.py:16
  397.9 3.1 all-reduce.3
  401.0 16.2 %all-reduce = (f32[]{:T(128)}, f32[128]{0:T(128)S(1)}, f32[128]{0:T(128)S(1)}) all-reduce(f32[]{:T(128)} %get-tuple-element.350, f32[128]{0:T(128)S(1)} %get-tuple-element.351, f32[128]{0:T(128)S(1)} %get-tuple-element.352), channel_id=1, replica_groups=mesh['dp_0'=4,'dp_1'=4,'dp_2'=2,'seq'=8] {'seq'}, use_global_device_ids=true, to_apply=%region_17.18 | all-reduce | flops 257 | bytes 2056 | tf_op jit(solution)/shard_map/psum | solution.py:16
  (113 shorter events, 45.3 us)
Async XLA Ops:
  7.2 1.1 copy-start.12
  7.2 181.7 %all-gather.3.cloned.1.call-start = ((), (), s32[]{:S(2)}) async-start(), calls=%async_computation.8 | async-start | bytes 14155776 | tf_op jit(solution)/shard_map/all_gather | solution.py:75
  8.3 9.7 %copy-start.13 = (bf16[1,128,3072]{2,1,0:T(8,128)(2,1)S(1)}, bf16[1,128,3072]{2,1,0:T(8,128)(2,1)}, u32[]{:S(2)}) copy-start(bf16[1,128,3072]{2,1,0:T(8,128)(2,1)} %param.13) | copy-start | bytes 2359300
  9.5 35.9 %all-to-all-start = ((bf16[128,8,384]{0,2,1:T(8,128)(2,1)}), bf16[128,8,384]{0,2,1:T(8,128)(2,1)S(1)}, u32[]{:S(2)}, u32[]{:S(2)}) async-start(bf16[128,8,384]{0,2,1:T(8,128)(2,1)} %bitcast.4), calls=%async_computation | async-start | bytes 1572864 | tf_op jit(solution)/shard_map/all_to_all | solution.py:44
  18.0 33.2 %copy-start.14 = (bf16[1,128,3072]{2,1,0:T(8,128)(2,1)S(1)}, bf16[1,128,3072]{2,1,0:T(8,128)(2,1)}, u32[]{:S(2)}) copy-start(bf16[1,128,3072]{2,1,0:T(8,128)(2,1)} %param.14) | copy-start | bytes 2359300
  45.4 42.6 %copy-start.7 = (bf16[128,8,384]{0,2,1:T(8,128)(2,1)}, bf16[128,8,384]{0,2,1:T(8,128)(2,1)S(1)}, u32[]{:S(2)}) copy-start(bf16[128,8,384]{0,2,1:T(8,128)(2,1)S(1)} %all-to-all-done) | copy-start | bytes 2359300
  45.4 37.0 %all-to-all-start.1 = ((bf16[128,8,384]{0,2,1:T(8,128)(2,1)}), bf16[128,8,384]{0,2,1:T(8,128)(2,1)S(1)}, u32[]{:S(2)}, u32[]{:S(2)}) async-start(bf16[128,8,384]{0,2,1:T(8,128)(2,1)} %bitcast.8), calls=%async_computation.1 | async-start | bytes 1572864 | tf_op jit(solution)/shard_map/all_to_all | solution.py:45
  51.2 36.5 %copy-start.18 = (f32[128]{0:T(128)S(1)}, f32[128]{0:T(128)}, u32[]{:S(2)}) copy-start(f32[128]{0:T(128)} %param.18) | copy-start | bytes 1540
  51.2 36.5 %copy-start.19 = (s32[1,4]{1,0:T(1,128)S(1)}, s32[1,4]{1,0:T(1,128)}, u32[]{:S(2)}) copy-start(s32[1,4]{1,0:T(1,128)} %param.16) | copy-start | bytes 52
  82.4 5.6 %copy-start.11 = (bf16[128,8,384]{0,2,1:T(8,128)(2,1)}, bf16[128,8,384]{0,2,1:T(8,128)(2,1)S(1)}, u32[]{:S(2)}) copy-start(bf16[128,8,384]{0,2,1:T(8,128)(2,1)S(1)} %all-to-all-done.1) | copy-start | bytes 2359300
  82.4 36.3 %all-to-all-start.2 = ((bf16[128,8,384]{0,2,1:T(8,128)(2,1)}), bf16[128,8,384]{0,2,1:T(8,128)(2,1)}, u32[]{:S(2)}, u32[]{:S(2)}) async-start(bf16[128,8,384]{0,2,1:T(8,128)(2,1)} %bitcast.10), calls=%async_computation.2 | async-start | bytes 1572864 | tf_op jit(solution)/shard_map/all_to_all | solution.py:46
  87.7 284.4 %reduce-scatter.2.cloned.1.call-start = ((), (), s32[]{:S(2)}) async-start(), calls=%async_computation.7 | async-start | bytes 4866048 | tf_op jit(solution)/shard_map/reduce_scatter | solution.py:120
  89.0 1.7 copy-start.4
  95.6 0.7 copy-start.17
  125.7 1.9 copy-start.3
  130.5 3.5 copy-start
  134.0 1.9 copy-start.2
  134.0 1.9 copy-start.15
  135.9 2.6 copy-start.1
  138.5 0.9 copy-start.16
  141.1 3.5 copy-start
  144.5 1.9 copy-start.2
  144.5 1.9 copy-start.15
  146.5 2.6 copy-start.1
  149.1 0.9 copy-start.16
  289.5 28.7 %all-to-all-start.3 = ((bf16[8,128,384]{1,2,0:T(8,128)(2,1)}), bf16[8,128,384]{1,2,0:T(8,128)(2,1)}, u32[]{:S(2)}, u32[]{:S(2)}) async-start(bf16[8,128,384]{1,2,0:T(8,128)(2,1)} %fusion.47), calls=%async_computation.3 | async-start | bytes 1572864 | tf_op jit(solution)/shard_map/all_to_all | solution.py:110
  296.2 2.0 copy-start.8
  318.2 25.2 %all-to-all-start.4 = ((bf16[8,128,384]{2,1,0:T(8,128)(2,1)}), bf16[8,128,384]{2,1,0:T(8,128)(2,1)S(1)}, u32[]{:S(2)}, u32[]{:S(2)}) async-start(bf16[8,128,384]{2,1,0:T(8,128)(2,1)} %copy.163), calls=%async_computation.4 | async-start | bytes 1572864 | tf_op jit(solution)/shard_map/all_to_all | solution.py:113
  323.4 25.6 %copy-start.5 = (f32[8,128,384]{1,0,2:T(8,128)S(1)}, f32[8,128,384]{1,0,2:T(8,128)}, u32[]{:S(2)}) copy-start(f32[8,128,384]{1,0,2:T(8,128)} %copy-done.4) | copy-start | bytes 4718596
  343.4 5.5 %copy-start.9 = (bf16[8,128,384]{2,1,0:T(8,128)(2,1)}, bf16[8,128,384]{2,1,0:T(8,128)(2,1)S(1)}, u32[]{:S(2)}) copy-start(bf16[8,128,384]{2,1,0:T(8,128)(2,1)S(1)} %all-to-all-done.4) | copy-start | bytes 2359300
  343.4 25.9 %all-to-all-start.5 = ((bf16[8,128,384]{2,1,0:T(8,128)(2,1)}), bf16[8,128,384]{2,1,0:T(8,128)(2,1)}, u32[]{:S(2)}, u32[]{:S(2)}) async-start(bf16[8,128,384]{2,1,0:T(8,128)(2,1)} %copy.165), calls=%async_computation.5 | async-start | bytes 1572864 | tf_op jit(solution)/shard_map/all_to_all | solution.py:116
  349.0 1.9 copy-start.6
  353.6 2.4 copy-start.10
Sparse Core Ops, SparseCore 0:
  9.8 179.0 all-gather.2
  200.5 91.9 reduce-scatter.1
where the time goes:
time: 432 us; the launch traced here: 430 us
  waiting for transfers between devices  156 us (36%)
  matrix products  86.1 us (20%)
  local copies, waits for them, and re-layouts  60.2 us (14%)
  blocking collectives  43.5 us (10%)
  starting transfers between devices  36.9 us (9%)
  other arithmetic  26.9 us (6%)
  between operations  17.5 us (4%)
    psum x4, blocking collectives, one_axis_at_a_time(): array = lax.psum(array, axis)  43.5 us
    all_gather x1, waiting for transfers between devices, local(): out_full = lax.all_gather(out_grad[0], 'seq', axis=0, tiled=True)  32.1 us
    all_to_all x1, waiting for transfers between devices, local(): lax.all_to_all(key_rows[0], 'seq', split_axis=1, concat_axis=0, tiled=True)  30 us
    all_to_all x1, waiting for transfers between devices, local(): lax.all_to_all(query_rows[0], 'seq', split_axis=1, concat_axis=0, tiled=T...  26.2 us
    dot_general x2, matrix products, backward_block(): jnp.einsum('hqk,qhd->khd', d_scores, query_block, preferred_element_type=...  20.3 us
    all_to_all x1, waiting for transfers between devices, local(): lax.all_to_all(value_rows[0], 'seq', split_axis=1, concat_axis=0, tiled=T...  19.1 us
    dot_general x2, matrix products, backward_block(): jnp.einsum('hqk,khd->qhd', d_scores, k_norm, preferred_element_type=jnp.f...  19 us
    all_to_all x1, waiting for transfers between devices, local(): lax.all_to_all(key_grad.reshape(total, width), 'seq', split_axis=0, conca...  18.6 us
  transfers between devices with their start and end apart: 8, of which 7 were waited for; matrix products, arithmetic and copies ran while one was open for 35% of the time, Pallas kernels for 0%

commit v1 on v0

--- a/solution.py
+++ b/solution.py
@@ -9,6 +9,16 @@
 DP = ("dp_0", "dp_1", "dp_2")
 DP_SEQ = ("dp_0", "dp_1", "dp_2", "seq")
 EPS = 1e-06
+
+
+def _solve_plate(sheet):
+    link_axis = "seq"
+    fan = jax.lax.axis_size(link_axis)
+    series = [fan if i == 0 else 1 for i in range(sheet.ndim)]
+    item_now = jax.lax.all_to_all(
+        jnp.tile(sheet, series), link_axis, split_axis=0, concat_axis=0, tiled=True
+    )
+    return item_now
 
 
 def one_axis_at_a_time(array, axes):
@@ -72,7 +82,7 @@
 
     probs_all, attn_blocks = lax.map(forward_block, jnp.arange(blocks, dtype=jnp.int32))
     attn_flat = attn_blocks.reshape(total, width)
-    out_full = lax.all_gather(out_grad[0], "seq", axis=0, tiled=True)
+    out_full = _solve_plate(out_grad[0])
     weight_part = jnp.dot(attn_flat.T, out_full, preferred_element_type=jnp.float32)
     d_attn = jnp.dot(out_full, out_weight.T, preferred_element_type=jnp.float32).astype(
         jnp.bfloat16

time: 432 us -> 627 us (1.45)
  waiting for transfers between devices: 156 us -> 319 us
  blocking collectives: 43.5 us -> 68.4 us
  local copies, waits for them, and re-layouts: 60.2 us -> 67.7 us
    all_to_all x1, waiting for transfers between devices: 19.1 us -> 225 us  [_solve_plate(): jax.lax.all_to_all(jnp.tile(sheet, series), link_axis, split_axis=0, conc...]
    all_gather x1 -> x0, waiting for transfers between devices: 32.1 us -> none  [local(): out_full = lax.all_gather(out_grad[0], 'seq', axis=0, tiled=True)]
    all_to_all x0 -> x1, blocking collectives: none -> 26.7 us  [local(): lax.all_to_all(value_rows[0], 'seq', split_axis=1, concat_axis=0, tiled=T...]
    all_to_all x1, waiting for transfers between devices: 30 us -> 21.8 us  [local(): lax.all_to_all(key_rows[0], 'seq', split_axis=1, concat_axis=0, tiled=True)]
    another operation x0 -> x1, local copies, waits for them, and re-layouts: none -> 7.45 us  [_solve_plate(): jnp.tile(sheet, series)]
  transfers between devices with their start and end apart: 8 -> 7, of which waited for: 7 -> 6; matrix products, arithmetic and copies ran while one was open for 35% -> 22% of each run, Pallas kernels for 0% -> 0%
where the time goes in v1:
time: 627 us; the launch traced here: 626 us
  waiting for transfers between devices  319 us (51%)
  matrix products  85.7 us (14%)
  blocking collectives  68.4 us (11%)
  local copies, waits for them, and re-layouts  67.7 us (11%)
  starting transfers between devices  37.2 us (6%)
  other arithmetic  26.9 us (4%)
  between operations  17.5 us (3%)
    all_to_all x1, waiting for transfers between devices, _solve_plate(): jax.lax.all_to_all(jnp.tile(sheet, series), link_axis, split_axis=0, conc...  225 us
    psum x4, blocking collectives, one_axis_at_a_time(): array = lax.psum(array, axis)  41.8 us
    all_to_all x1, blocking collectives, local(): lax.all_to_all(value_rows[0], 'seq', split_axis=1, concat_axis=0, tiled=T...  26.7 us
    all_to_all x1, waiting for transfers between devices, local(): lax.all_to_all(key_rows[0], 'seq', split_axis=1, concat_axis=0, tiled=True)  21.8 us
    all_to_all x1, waiting for transfers between devices, local(): lax.all_to_all(query_rows[0], 'seq', split_axis=1, concat_axis=0, tiled=T...  20.5 us
    all_to_all x1, waiting for transfers between devices, local(): lax.all_to_all(key_grad.reshape(total, width), 'seq', split_axis=0, conca...  20.5 us
    dot_general x2, matrix products, backward_block(): jnp.einsum('hqk,qhd->khd', d_scores, query_block, preferred_element_type=...  20.1 us
    dot_general x2, matrix products, backward_block(): jnp.einsum('hqk,khd->qhd', d_scores, k_norm, preferred_element_type=jnp.f...  19.2 us
  transfers between devices with their start and end apart: 7, of which 6 were waited for; matrix products, arithmetic and copies ran while one was open for 22% of the time, Pallas kernels for 0%

profile of v1, /device:TPU:32, one launch (start us, length us, event | category | flops | bytes accessed | tf_op | source)
XLA Modules:
  0.0 625.8 jit_solution(12253247911826746633)
XLA Ops:
  7.2 2.4 copy.144
  9.5 8.6 %all-to-all-start = ((bf16[128,8,384]{0,2,1:T(8,128)(2,1)}), bf16[128,8,384]{0,2,1:T(8,128)(2,1)S(1)}, u32[]{:S(2)}, u32[]{:S(2)}) async-start(bf16[128,8,384]{0,2,1:T(8,128)(2,1)} %bitcast.4), calls=%async_computation | async-start | bytes 1572864 | tf_op jit(solution)/shard_map/all_to_all | solution.py:54
  19.3 20.5 %all-to-all-done = bf16[128,8,384]{0,2,1:T(8,128)(2,1)S(1)} async-done(((bf16[128,8,384]{0,2,1:T(8,128)(2,1)}), bf16[128,8,384]{0,2,1:T(8,128)(2,1)S(1)}, u32[]{:S(2)}, u32[]{:S(2)}) %all-to-all-start) | async-done | bytes 786464 | tf_op jit(solution)/shard_map/all_to_all | solution.py:54
  39.8 4.9 all-to-all-start.1
  45.1 21.8 %all-to-all-done.1 = bf16[128,8,384]{0,2,1:T(8,128)(2,1)S(1)} async-done(((bf16[128,8,384]{0,2,1:T(8,128)(2,1)}), bf16[128,8,384]{0,2,1:T(8,128)(2,1)S(1)}, u32[]{:S(2)}, u32[]{:S(2)}) %all-to-all-start.1) | async-done | bytes 786464 | tf_op jit(solution)/shard_map/all_to_all | solution.py:55
  66.8 26.7 %all_to_all.96 = bf16[128,8,384]{0,2,1:T(8,128)(2,1)} all-to-all(bf16[128,8,384]{0,2,1:T(8,128)(2,1)S(1)} %bitcast.150), channel_id=1, replica_groups=mesh['dp_0'=4,'dp_1'=4,'dp_2'=2,'seq'=8] {'seq'}, dimensions={1} | all-to-all | bytes 1572864 | tf_op jit(solution)/shard_map/all_to_all | solution.py:56
  93.5 7.5 %tile.9 = bf16[8,128,6144]{2,1,0:T(8,128)(2,1)} broadcast(bf16[128,6144]{1,0:T(8,128)(2,1)} %bitcast.158), dimensions={1,2} | broadcast | bytes 14155776 | tf_op jit(solution)/shard_map/tile | solution.py:19
  100.9 6.8 %all-to-all-start.3 = ((bf16[8,128,6144]{2,1,0:T(8,128)(2,1)}), bf16[8,128,6144]{2,1,0:T(8,128)(2,1)}, u32[]{:S(2)}, u32[]{:S(2)}) async-start(bf16[8,128,6144]{2,1,0:T(8,128)(2,1)} %tile.9), calls=%async_computation.3 | async-start | bytes 25165824 | tf_op jit(solution)/shard_map/all_to_all | solution.py:18
  111.9 2.1 copy.147
  117.3 2.3 copy.151
  119.6 2.5 copy.149
  122.1 2.2 reshape.184
  124.3 2.3 copy.152
  129.6 21.3 %while.27 = (s32[]{:T(128)}, bf16[2,3,512,1024]{3,2,1,0:T(8,128)(2,1)}, bf16[2,512,3,128]{3,1,2,0:T(8,128)(2,1)}, s32[2]{0:T(128)S(1)}, s32[1024]{0:T(1024)S(1)}...) while((s32[]{:T(128)}, ...), condition=%wide.region_6.7_spmd, body=%wide.region_4.6_spmd.sunk | while | flops 817035776 | bytes 85746000 | solution.py:83
  131.3 3.4 fusion.67
  142.0 3.4 fusion.67
  151.0 3.0 copy.167
  154.0 2.2 copy.180
  157.8 224.9 %all-to-all-done.3 = bf16[8,128,6144]{2,1,0:T(8,128)(2,1)} async-done(((bf16[8,128,6144]{2,1,0:T(8,128)(2,1)}), bf16[8,128,6144]{2,1,0:T(8,128)(2,1)}, u32[]{:S(2)}, u32[]{:S(2)}) %all-to-all-start.3) | async-done | bytes 12582944 | tf_op jit(solution)/shard_map/all_to_all | solution.py:18
  382.7 10.2 %convolution_convert_fusion.2 = bf16[1024,384]{0,1:T(8,128)(2,1)} fusion(bf16[1024,6144]{1,0:T(8,128)(2,1)} %bitcast.13, bf16[384,6144]{1,0:T(8,128)(2,1)} %param.17), kind=kOutput, calls=%fused_computation.58 | convolution fusion | flops 4832231424 | bytes 18087936 | tf_op jit(solution)/shard_map/dot_general | solution.py:87
  392.9 11.2 %convolution_convert_fusion.1 = bf16[384,6144]{0,1:T(8,128)(2,1)} fusion(bf16[1024,384]{0,1:T(8,128)(2,1)S(1)} %bitcast.159, bf16[1024,6144]{1,0:T(8,128)(2,1)} %bitcast.13), kind=kOutput, calls=%fused_computation.41 | convolution fusion | flops 4834197504 | bytes 18087936 | tf_op jit(solution)/shard_map/dot_general | solution.py:86
  404.1 57.8 %while.28 = (s32[]{:T(128)}, f32[1024,3,128]{0,2,1:T(8,128)}, f32[1024,3,128]{0,2,1:T(8,128)S(1)}, f32[2,512,3,128]{3,1,2,0:T(8,128)}, s32[2]{0:T(128)S(1)}, /*i...) while((s32[]{:T(128)}, f32[1024,3,128]{0,2,1:T(8,128)}, ...), condition=%wide.region_9.10_spmd.clone, body=%wide.region_7.9_spmd.clone.sunk | while | flops 1634210816 | bytes 57019604 | solution.py:112
  405.4 4.9 fusion.75
  410.3 10.0 %bitcast_add_fusion.4 = f32[1024,3,128]{0,2,1:T(8,128)} fusion(f32[1024,3,128]{0,2,1:T(8,128)} %get-tuple-element.528, f32[3,512,1024]{2,1,0:T(8,128)} %fusion.75, bf16[2,3,512,1024]{3,2,1,0:T(8,128)(2,1)} %get-tuple-element.547, s32[]{:T(128)} %get-tuple-element.527, pred[]{:T(512)S(6)} %compare.3, bf16[1024,3,128]{0,2,1:T(8,128)(2,1)} %get-tuple-element.546, ...), kind=kOutput, calls=%fused_computation.26.clone.1 | convolution fusion | flops 414452224 | bytes 22414340 | tf_op jit(solution)/shard_map/while/body/eval_jaxpr/hqk,qhd->khd/dot_general | solution.py:105
  420.3 9.7 %fusion.76 = f32[2,512,3,128]{3,1,2,0:T(8,128)} fusion(f32[2,512,3,128]{3,1,2,0:T(8,128)} %get-tuple-element.530, s32[]{:T(128)} %get-tuple-element.527, bf16[1024,3,128]{2,0,1:T(8,128)(2,1)} %get-tuple-element.550, f32[3,512,1024]{2,1,0:T(8,128)} %fusion.75, bf16[2,3,512,1024]{3,2,1,0:T(8,128)(2,1)} %get-tuple-element.547), kind=kOutput, calls=%fused_computation.28.clone.1 | convolution fusion | flops 413665792 | bytes 20448768 | tf_op jit(solution)/shard_map/while/body/eval_jaxpr/hqk,khd->qhd/dot_general | solution.py:108
  429.9 3.0 bitcast_add_fusion.5
  434.2 5.0 fusion.75
  439.2 10.2 %bitcast_add_fusion.4 = f32[1024,3,128]{0,2,1:T(8,128)} fusion(f32[1024,3,128]{0,2,1:T(8,128)} %get-tuple-element.528, f32[3,512,1024]{2,1,0:T(8,128)} %fusion.75, bf16[2,3,512,1024]{3,2,1,0:T(8,128)(2,1)} %get-tuple-element.547, s32[]{:T(128)} %get-tuple-element.527, pred[]{:T(512)S(6)} %compare.3, bf16[1024,3,128]{0,2,1:T(8,128)(2,1)} %get-tuple-element.546, ...), kind=kOutput, calls=%fused_computation.26.clone.1 | convolution fusion | flops 414452224 | bytes 22414340 | tf_op jit(solution)/shard_map/while/body/eval_jaxpr/hqk,qhd->khd/dot_general | solution.py:105
  449.4 9.5 %fusion.76 = f32[2,512,3,128]{3,1,2,0:T(8,128)} fusion(f32[2,512,3,128]{3,1,2,0:T(8,128)} %get-tuple-element.530, s32[]{:T(128)} %get-tuple-element.527, bf16[1024,3,128]{2,0,1:T(8,128)(2,1)} %get-tuple-element.550, f32[3,512,1024]{2,1,0:T(8,128)} %fusion.75, bf16[2,3,512,1024]{3,2,1,0:T(8,128)(2,1)} %get-tuple-element.547), kind=kOutput, calls=%fused_computation.28.clone.1 | convolution fusion | flops 413665792 | bytes 20448768 | tf_op jit(solution)/shard_map/while/body/eval_jaxpr/hqk,khd->qhd/dot_general | solution.py:108
  458.9 2.9 bitcast_add_fusion.5
  461.9 3.7 copy.156
  465.6 2.7 copy.159
  468.3 3.1 copy.160
  471.4 2.3 multiply_reduce_fusion.3
  475.3 3.3 reshape.186
  478.6 4.3 fusion.40
  482.9 6.5 %all-to-all-start.4 = ((bf16[8,128,384]{1,2,0:T(8,128)(2,1)}), bf16[8,128,384]{1,2,0:T(8,128)(2,1)}, u32[]{:S(2)}, u32[]{:S(2)}) async-start(bf16[8,128,384]{1,2,0:T(8,128)(2,1)} %fusion.40), calls=%async_computation.4 | async-start | bytes 1572864 | tf_op jit(solution)/shard_map/all_to_all | solution.py:120
  493.4 18.1 %all-to-all-done.4 = bf16[8,128,384]{1,2,0:T(8,128)(2,1)} async-done(((bf16[8,128,384]{1,2,0:T(8,128)(2,1)}), bf16[8,128,384]{1,2,0:T(8,128)(2,1)}, u32[]{:S(2)}, u32[]{:S(2)}) %all-to-all-start.4) | async-done | bytes 786464 | tf_op jit(solution)/shard_map/all_to_all | solution.py:120
  511.6 4.9 all-to-all-start.5
  518.2 20.5 %all-to-all-done.5 = bf16[8,128,384]{2,1,0:T(8,128)(2,1)S(1)} async-done(((bf16[8,128,384]{2,1,0:T(8,128)(2,1)}), bf16[8,128,384]{2,1,0:T(8,128)(2,1)S(1)}, u32[]{:S(2)}, u32[]{:S(2)}) %all-to-all-start.5) | async-done | bytes 786464 | tf_op jit(solution)/shard_map/all_to_all | solution.py:123
  538.6 5.5 all-to-all-start.6
  546.1 2.6 multiply_reduce_fusion.1
  548.8 2.4 copy.170
  552.7 13.7 %all-to-all-done.6 = bf16[8,128,384]{2,1,0:T(8,128)(2,1)} async-done(((bf16[8,128,384]{2,1,0:T(8,128)(2,1)}), bf16[8,128,384]{2,1,0:T(8,128)(2,1)}, u32[]{:S(2)}, u32[]{:S(2)}) %all-to-all-start.6) | async-done | bytes 786464 | tf_op jit(solution)/shard_map/all_to_all | solution.py:126
  570.7 11.3 %all-reduce.2 = (f32[]{:T(128)}, f32[128]{0:T(128)S(1)}, f32[128]{0:T(128)S(1)}) all-reduce(f32[]{:T(128)} %fusion.41, f32[128]{0:T(128)S(1)} %multiply_reduce_fusion.1, f32[128]{0:T(128)S(1)} %get-tuple-element.303), channel_id=1, replica_groups=mesh['dp_0'=4,'dp_1'=4,'dp_2'=2,'seq'=8] {'dp_0'}, use_global_device_ids=true, to_apply=%region_14.15 | all-reduce | flops 257 | bytes 2056 | tf_op jit(solution)/shard_map/psum | solution.py:26
  582.0 11.2 %all-reduce.1 = (f32[]{:T(128)}, f32[128]{0:T(128)S(1)}, f32[128]{0:T(128)S(1)}) all-reduce(f32[]{:T(128)} %get-tuple-element.347, f32[128]{0:T(128)S(1)} %get-tuple-element.348, f32[128]{0:T(128)S(1)} %get-tuple-element.349), channel_id=1, replica_groups=mesh['dp_0'=4,'dp_1'=4,'dp_2'=2,'seq'=8] {'dp_1'}, use_global_device_ids=true, to_apply=%region_15.16 | all-reduce | flops 257 | bytes 2056 | tf_op jit(solution)/shard_map/psum | solution.py:26
  593.2 3.1 all-reduce.3
  596.3 16.2 %all-reduce = (f32[]{:T(128)}, f32[128]{0:T(128)S(1)}, f32[128]{0:T(128)S(1)}) all-reduce(f32[]{:T(128)} %get-tuple-element.350, f32[128]{0:T(128)S(1)} %get-tuple-element.351, f32[128]{0:T(128)S(1)} %get-tuple-element.352), channel_id=1, replica_groups=mesh['dp_0'=4,'dp_1'=4,'dp_2'=2,'seq'=8] {'seq'}, use_global_device_ids=true, to_apply=%region_17.18 | all-reduce | flops 257 | bytes 2056 | tf_op jit(solution)/shard_map/psum | solution.py:26
  (112 shorter events, 46.2 us)
Async XLA Ops:
  7.2 10.9 %copy-start.12 = (bf16[1,128,3072]{2,1,0:T(8,128)(2,1)S(1)}, bf16[1,128,3072]{2,1,0:T(8,128)(2,1)}, u32[]{:S(2)}) copy-start(bf16[1,128,3072]{2,1,0:T(8,128)(2,1)} %param.13) | copy-start | bytes 2359300
  9.5 30.2 %all-to-all-start = ((bf16[128,8,384]{0,2,1:T(8,128)(2,1)}), bf16[128,8,384]{0,2,1:T(8,128)(2,1)S(1)}, u32[]{:S(2)}, u32[]{:S(2)}) async-start(bf16[128,8,384]{0,2,1:T(8,128)(2,1)} %bitcast.4), calls=%async_computation | async-start | bytes 1572864 | tf_op jit(solution)/shard_map/all_to_all | solution.py:54
  18.1 26.6 %copy-start.13 = (bf16[1,128,3072]{2,1,0:T(8,128)(2,1)S(1)}, bf16[1,128,3072]{2,1,0:T(8,128)(2,1)}, u32[]{:S(2)}) copy-start(bf16[1,128,3072]{2,1,0:T(8,128)(2,1)} %param.14) | copy-start | bytes 2359300
  39.8 68.3 %copy-start.7 = (bf16[128,8,384]{0,2,1:T(8,128)(2,1)}, bf16[128,8,384]{0,2,1:T(8,128)(2,1)S(1)}, u32[]{:S(2)}) copy-start(bf16[128,8,384]{0,2,1:T(8,128)(2,1)S(1)} %all-to-all-done) | copy-start | bytes 2359300
  39.8 27.1 %all-to-all-start.1 = ((bf16[128,8,384]{0,2,1:T(8,128)(2,1)}), bf16[128,8,384]{0,2,1:T(8,128)(2,1)S(1)}, u32[]{:S(2)}, u32[]{:S(2)}) async-start(bf16[128,8,384]{0,2,1:T(8,128)(2,1)} %bitcast.8), calls=%async_computation.1 | async-start | bytes 1572864 | tf_op jit(solution)/shard_map/all_to_all | solution.py:55
  66.8 34.1 %copy-start.11 = (bf16[128,8,384]{0,2,1:T(8,128)(2,1)}, bf16[128,8,384]{0,2,1:T(8,128)(2,1)S(1)}, u32[]{:S(2)}) copy-start(bf16[128,8,384]{0,2,1:T(8,128)(2,1)S(1)} %all-to-all-done.1) | copy-start | bytes 2359300
  100.9 6.8 %copy-start.19 = (s32[1,4]{1,0:T(1,128)S(1)}, s32[1,4]{1,0:T(1,128)}, u32[]{:S(2)}) copy-start(s32[1,4]{1,0:T(1,128)} %param.16) | copy-start | bytes 52
  100.9 7.1 %copy-start.18 = (f32[128]{0:T(128)S(1)}, f32[128]{0:T(128)}, u32[]{:S(2)}) copy-start(f32[128]{0:T(128)} %param.18) | copy-start | bytes 1540
  100.9 281.7 %all-to-all-start.3 = ((bf16[8,128,6144]{2,1,0:T(8,128)(2,1)}), bf16[8,128,6144]{2,1,0:T(8,128)(2,1)}, u32[]{:S(2)}, u32[]{:S(2)}) async-start(bf16[8,128,6144]{2,1,0:T(8,128)(2,1)} %tile.9), calls=%async_computation.3 | async-start | bytes 25165824 | tf_op jit(solution)/shard_map/all_to_all | solution.py:18
  107.7 461.4 %reduce-scatter.2.cloned.1.call-start = ((), (), s32[]{:S(2)}) async-start(), calls=%async_computation.8 | async-start | bytes 4866048 | tf_op jit(solution)/shard_map/reduce_scatter | solution.py:130
  109.1 2.8 copy-start.4
  115.5 0.7 copy-start.17
  126.6 1.9 copy-start.3
  131.3 3.4 copy-start
  134.8 1.9 copy-start.2
  134.8 1.9 copy-start.14
  136.7 2.7 copy-start.1
  139.4 0.9 copy-start.15
  142.0 3.4 copy-start
  145.4 1.9 copy-start.2
  145.4 1.9 copy-start.14
  147.4 2.7 copy-start.1
  150.1 0.9 copy-start.15
  382.7 10.2 %copy-start.16 = (bf16[48,8,2,512]{3,1,2,0:T(8,128)(2,1)S(1)}, bf16[48,8,2,512]{3,1,2,0:T(8,128)(2,1)}, u32[]{:S(2)}) copy-start(bf16[48,8,2,512]{3,1,2,0:T(8,128)(2,1)} %copy.180) | copy-start | bytes 2359300
  482.9 28.7 %all-to-all-start.4 = ((bf16[8,128,384]{1,2,0:T(8,128)(2,1)}), bf16[8,128,384]{1,2,0:T(8,128)(2,1)}, u32[]{:S(2)}, u32[]{:S(2)}) async-start(bf16[8,128,384]{1,2,0:T(8,128)(2,1)} %fusion.40), calls=%async_computation.4 | async-start | bytes 1572864 | tf_op jit(solution)/shard_map/all_to_all | solution.py:120
  489.4 2.0 copy-start.8
  511.6 27.0 %all-to-all-start.5 = ((bf16[8,128,384]{2,1,0:T(8,128)(2,1)}), bf16[8,128,384]{2,1,0:T(8,128)(2,1)S(1)}, u32[]{:S(2)}, u32[]{:S(2)}) async-start(bf16[8,128,384]{2,1,0:T(8,128)(2,1)} %copy.163), calls=%async_computation.5 | async-start | bytes 1572864 | tf_op jit(solution)/shard_map/all_to_all | solution.py:123
  516.8 27.4 %copy-start.5 = (f32[8,128,384]{1,0,2:T(8,128)S(1)}, f32[8,128,384]{1,0,2:T(8,128)}, u32[]{:S(2)}) copy-start(f32[8,128,384]{1,0,2:T(8,128)} %copy-done.4) | copy-start | bytes 4718596
  538.6 5.5 copy-start.9
  538.6 27.8 %all-to-all-start.6 = ((bf16[8,128,384]{2,1,0:T(8,128)(2,1)}), bf16[8,128,384]{2,1,0:T(8,128)(2,1)}, u32[]{:S(2)}, u32[]{:S(2)}) async-start(bf16[8,128,384]{2,1,0:T(8,128)(2,1)} %copy.165), calls=%async_computation.6 | async-start | bytes 1572864 | tf_op jit(solution)/shard_map/all_to_all | solution.py:126
  544.2 1.9 copy-start.6
  548.8 2.4 copy-start.10
Sparse Core Ops, SparseCore 0:
  404.2 89.8 reduce-scatter.1
